TPU v7x, 512 devices: a 8x2x16 block of a 8x8x16 slice. The times are simulated.
512 devices in a mesh: groups: 2 (over y), seq: 16 (over z), exp: 8 (over x), tp: 2 (over core).
Axes of the slice: x: 8, y: 2, z: 16, core: 2. Of those that a mesh axis runs over, the one named last changes fastest.
The devices are a block of a 8x8x16 slice.
Arguments:
- attn_query: bfloat16 [8192, 1152], P(('groups', 'seq'), ('exp', 'tp')), parts along dimension 0, may hold values from -6 to 6
- fresh_keys: bfloat16 [8192, 1152], P(('groups', 'seq'), ('exp', 'tp')), parts along dimension 0, may hold values from -6 to 6
- fresh_values: bfloat16 [8192, 1152], P(('groups', 'seq'), ('exp', 'tp')), parts along dimension 0, may hold values from -6 to 6
- stale_keys: bfloat16 [8192, 1152], P(('groups', 'seq'), ('exp', 'tp')), parts along dimension 0, may hold values from -6 to 6
- stale_values: bfloat16 [8192, 1152], P(('groups', 'seq'), ('exp', 'tp')), parts along dimension 0, may hold values from -6 to 6
- block_flags: int32 [64], P(('groups', 'seq')), parts along dimension 0, may hold values 0 or 1
- moe_tokens: bfloat16 [65536, 1152], P(('groups', 'seq', 'exp', 'tp')), parts along dimension 0, may hold values from -6 to 6
- expert_ids: int32 [65536, 2], P(('groups', 'seq', 'exp', 'tp')), parts along dimension 0, may hold values from 0 to 15, all different within a row; in each aligned block of 128 rows (0 to 127, 128 to 255, ...) at most 20 rows name the same one
- gate_weights: float32 [65536, 2], P(('groups', 'seq', 'exp', 'tp')), parts along dimension 0, may hold values from 0.25 to 1
- up_weight: bfloat16 [16, 1152, 4608], P('seq', None, ('exp', 'tp')), may hold values from -0.1875 to 0.1875
- up_bias: float32 [16, 4608], P('seq', ('exp', 'tp')), may hold values from -3 to 3
- down_weight: bfloat16 [16, 4608, 1152], P('seq', ('exp', 'tp')), may hold values from -0.09375 to 0.09375
- down_bias: float32 [16, 1152], P('seq'), may hold values from -2 to 2
Outputs:
- attn_out: bfloat16 [8192, 1152], P(('groups', 'seq'), ('exp', 'tp')), parts along dimension 0
- moe_out: bfloat16 [65536, 1152], P(('groups', 'seq', 'exp', 'tp')), parts along dimension 0
There are 2 independent parts, one for each index of `groups`. A program takes and returns all parts, laid end to end along the dimension named above; an argument that names none is the same for every part. Nothing has to cross between parts.
Inputs may be any that keep to these rules, and one draw needn't show every extreme that they name: `expert_ids`: the 2 ids of a token differ. In the rows of one device no expert is named more than 20 times, and in every draw some expert is named exactly 20 times in some device's rows.
All inputs are finite; a program needn't handle non-finite values. No bound on the sum of `block_flags` on one device may be relied on, other than what follows from the above.
Results may differ from a plain program's by a relative error of at most 0.014.
Values may be sent and summed in bfloat16 or wider, within the bound.
No kernel may reach another device: no remote copies, remote signals or barrier semaphores. Data moves between devices by JAX's collectives and lax.ppermute only.
A program may use at most 64 MiB of HBM per device.

v0:
```python
import math
import jax
import jax.numpy as jnp
from jax import lax
from jax.sharding import PartitionSpec as P

HD = 72


def in_one_piece(arrays, axis, dim, along):
    widths = [a.shape[along] for a in arrays]
    both = jnp.concatenate(arrays, axis=along)
    result = lax.all_gather(both, axis, axis=dim, tiled=True)
    return tuple(jnp.split(result, [sum(widths[:k]) for k in range(1, len(widths))], axis=along))


def sent_to_all(value, axis):
    copies = jnp.broadcast_to(value, (lax.axis_size(axis), *value.shape))
    return lax.all_to_all(copies, axis, split_axis=0, concat_axis=0, tiled=True)


def laid_out(parts, dim):
    parts = jnp.moveaxis(parts, 0, dim)
    dims = parts.shape
    return parts.reshape(*dims[:dim], dims[dim] * dims[dim + 1], *dims[dim + 2 :])


def collect(value, axis, dim):
    parts = sent_to_all(value, axis)
    return laid_out(parts, dim)


def over_all(share, axis, dim, apply):
    everything = lax.all_gather(share, axis, axis=dim, tiled=True)
    return apply(everything, jnp.int32(0))


def in_blocks(value, dim, size):
    dims = value.shape
    parts = value.reshape(*dims[:dim], size, dims[dim] // size, *dims[dim + 1 :])
    return jnp.moveaxis(parts, dim, 0)


def summed_on_arrival(value, axis, dim):
    size = lax.axis_size(axis)
    parts = lax.all_to_all(in_blocks(value, dim, size), axis, 0, 0, tiled=True)
    return jnp.sum(parts.astype(jnp.float32), axis=0)


def grouped_exchange(value, axis, split_dim, concat_dim, work, item_dim, out_dim):

    def moved(group):
        return lax.all_to_all(group, axis, split_axis=split_dim, concat_axis=concat_dim, tiled=True)

    items = jax.tree.leaves(value)[0].shape[item_dim]
    ends = [items * k // 2 for k in range(2 + 1)] if items % 2 == 0 else [0, items]
    groups = [
        jax.tree.map(lambda a: lax.slice_in_dim(a, low, high, axis=item_dim), value)
        for low, high in zip(ends, ends[1:])
    ]
    arrived = [moved(group) for group in groups]
    made = [work(group) for group in arrived]
    return jax.tree.map(lambda *parts: jnp.concatenate(parts, axis=out_dim), *made)


def attention_part(attn_query, fresh_keys, fresh_values, stale_keys, stale_values, block_flags):
    length = attn_query.shape[0]
    heads_here = attn_query.shape[1] // HD
    row_flags = (jnp.repeat(block_flags, length // block_flags.shape[0]) == 1)[:, None]
    keys = jnp.where(row_flags, fresh_keys, stale_keys)
    values = jnp.where(row_flags, fresh_values, stale_values)
    queries = attn_query.reshape(length, heads_here, HD)
    scale = 1.0 / math.sqrt(HD)
    initial = (
        jnp.full((heads_here, length), -1e30, jnp.float32),
        jnp.zeros((heads_here, length), jnp.float32),
        jnp.zeros((heads_here, length, HD), jnp.float32),
    )
    carry = initial
    piece = in_one_piece((keys, values), "seq", 0, 1)
    count = piece[0].shape[0]
    width = math.gcd(count, 512)
    key_blocks = piece[0].reshape(count // width, width, heads_here, HD)
    value_blocks = piece[1].reshape(count // width, width, heads_here, HD)

    def advance(state, blocks):
        highest, totals, weighted = state
        key_block, value_block = blocks
        scores = (
            jnp.einsum("qhd,khd->hqk", queries, key_block, preferred_element_type=jnp.float32)
            * scale
        )
        new_high = jnp.maximum(highest, jnp.max(scores, axis=-1))
        rescale = jnp.exp(highest - new_high)
        probs = jnp.exp(scores - new_high[:, :, None])
        totals = totals * rescale + jnp.sum(probs, axis=-1)
        weighted = weighted * rescale[:, :, None] + jnp.einsum(
            "hqk,khd->hqd",
            probs.astype(jnp.bfloat16),
            value_block,
            preferred_element_type=jnp.float32,
        )
        return ((new_high, totals, weighted), None)

    carry, unused = lax.scan(advance, carry, (key_blocks, value_blocks))
    highest, totals, weighted = carry
    mixed = weighted / totals[:, :, None]
    return jnp.transpose(mixed, (1, 0, 2)).reshape(length, heads_here * HD).astype(jnp.bfloat16)


def expert_part(moe_tokens, expert_ids, gate_weights, up_weight, up_bias, down_weight, down_bias):
    tokens_here, width = moe_tokens.shape
    choose = expert_ids.shape[1]
    number = lax.axis_size("seq") * up_weight.shape[0]
    capacity = 5 * tokens_here // (2 * number)
    flat_ids = expert_ids.reshape(-1)
    hits = (flat_ids[:, None] == jnp.arange(number, dtype=jnp.int32)[None, :]).astype(jnp.int32)
    before = jnp.cumsum(hits, axis=0) - hits
    place = jnp.sum(before * hits, axis=1)
    slot = flat_ids * capacity + place
    slot_pairs = slot.reshape(tokens_here, choose)
    table = jnp.sum(
        (
            slot_pairs[None, :, :] == jnp.arange(number * capacity, dtype=jnp.int32)[:, None, None]
        ).astype(jnp.int32),
        axis=-1,
    )
    buffer = jnp.dot(
        table.astype(jnp.bfloat16), moe_tokens, preferred_element_type=jnp.float32
    ).astype(jnp.bfloat16)
    buffer = buffer.reshape(number, capacity, width)

    def expert_fn(received):
        sources, count = (received.shape[0], received.shape[1])
        flat_rows = received.reshape(sources * count, width)
        chip_rows = collect(flat_rows, "tp", 0)
        total_rows = chip_rows.shape[0]

        def project(piece):
            return jax.nn.gelu(
                jnp.dot(chip_rows, piece[0], preferred_element_type=jnp.float32) + piece[1]
            ).astype(jnp.bfloat16)

        hidden = over_all(
            (up_weight[0], up_bias[0][None, :].astype(jnp.bfloat16)),
            "exp",
            1,
            lambda piece, start: project((piece[0], piece[1].astype(jnp.float32))),
        )
        down_whole = lax.all_gather(down_weight[0], "exp", axis=0, tiled=True)
        hidden_rows = lax.slice_in_dim(
            hidden, 0, total_rows // lax.axis_size("tp") * lax.axis_size("tp"), axis=0
        )
        summed = summed_on_arrival(
            jnp.dot(hidden_rows, down_whole, preferred_element_type=jnp.float32).astype(
                jnp.bfloat16
            ),
            "tp",
            0,
        )
        result = (
            (summed + down_bias[0][None, :]).astype(jnp.bfloat16).reshape(sources, count, width)
        )
        return lax.all_to_all(result, "seq", split_axis=0, concat_axis=0, tiled=True)

    returned = grouped_exchange(buffer, "seq", 0, 0, expert_fn, 1, 1)
    flat_out = returned.reshape(number * capacity, width)
    picked = flat_out[slot].reshape(tokens_here, choose, width).astype(jnp.float32)
    combined = jnp.sum(picked * gate_weights[:, :, None], axis=1)
    return combined.astype(jnp.bfloat16)


def local(
    attn_query,
    fresh_keys,
    fresh_values,
    stale_keys,
    stale_values,
    block_flags,
    moe_tokens,
    expert_ids,
    gate_weights,
    up_weight,
    up_bias,
    down_weight,
    down_bias,
):
    attn_out = attention_part(
        attn_query, fresh_keys, fresh_values, stale_keys, stale_values, block_flags
    )
    moe_out = expert_part(
        moe_tokens, expert_ids, gate_weights, up_weight, up_bias, down_weight, down_bias
    )
    return (attn_out, moe_out)


def solution(mesh):
    in_specs = (
        P(("groups", "seq"), ("exp", "tp")),
        P(("groups", "seq"), ("exp", "tp")),
        P(("groups", "seq"), ("exp", "tp")),
        P(("groups", "seq"), ("exp", "tp")),
        P(("groups", "seq"), ("exp", "tp")),
        P(("groups", "seq")),
        P(("groups", "seq", "exp", "tp"), None),
        P(("groups", "seq", "exp", "tp"), None),
        P(("groups", "seq", "exp", "tp"), None),
        P("seq", None, ("exp", "tp")),
        P("seq", ("exp", "tp")),
        P("seq", ("exp", "tp"), None),
        P("seq", None),
    )
    out_specs = (P(("groups", "seq"), ("exp", "tp")), P(("groups", "seq", "exp", "tp"), None))
    return jax.shard_map(local, mesh=mesh, in_specs=in_specs, out_specs=out_specs, check_vma=False)
```

profile of v0, /device:TPU:68, one launch (start us, length us, event | category | flops | bytes accessed | tf_op | source)
XLA Modules:
  0.0 323.5 jit_solution(15727244440906299351)
XLA Ops:
  12.7 78.3 %all_to_all.40 = bf16[16,10,1152]{2,1,0:T(8,128)(2,1)S(1)} all-to-all(bf16[16,10,1152]{2,1,0:T(8,128)(2,1)S(1)} %get-tuple-element.100), channel_id=1, replica_groups=mesh['groups'=2,'seq'=16,'exp'=8,'tp'=2] {'seq'}, dimensions={0} | all-to-all | bytes 737280 | tf_op jit(solution)/shard_map/all_to_all | solution.py:53
  91.0 4.0 %all-to-all-start.4 = ((bf16[16,10,1152]{2,1,0:T(8,128)(2,1)}), bf16[16,10,1152]{2,1,0:T(8,128)(2,1)S(1)}, u32[]{:S(2)}, u32[]{:S(2)}) async-start(bf16[16,10,1152]{2,1,0:T(8,128)(2,1)} %get-tuple-element.101), calls=%async_computation.4 | async-start | bytes 1179648 | tf_op jit(solution)/shard_map/all_to_all | solution.py:53
  95.9 1.3 dynamic-slice
  98.2 16.6 %all-reduce = bf16[2304]{0:T(1024)(128)(2,1)S(1)} all-reduce(bf16[2304]{0:T(1024)(128)(2,1)S(1)} %dynamic-update-slice), channel_id=1, replica_groups=mesh['groups'=2,'seq'=16,'exp'=8,'tp'=2] {'exp'}, use_global_device_ids=true, to_apply=%add | all-reduce | flops 2304 | bytes 9216
  115.0 9.9 %all-to-all-done.4 = bf16[16,10,1152]{2,1,0:T(8,128)(2,1)S(1)} async-done(((bf16[16,10,1152]{2,1,0:T(8,128)(2,1)}), bf16[16,10,1152]{2,1,0:T(8,128)(2,1)S(1)}, u32[]{:S(2)}, u32[]{:S(2)}) %all-to-all-start.4) | async-done | bytes 368672 | tf_op jit(solution)/shard_map/all_to_all | solution.py:53
  125.8 3.6 %all-to-all-start.1 = ((bf16[2,160,1152]{2,1,0:T(8,128)(2,1)}), bf16[2,160,1152]{2,1,0:T(8,128)(2,1)S(1)}, u32[]{:S(2)}, u32[]{:S(2)}) async-start(bf16[2,160,1152]{2,1,0:T(8,128)(2,1)} %broadcast_in_dim.42), calls=%async_computation.1 | async-start | bytes 1474560 | tf_op jit(solution)/shard_map/all_to_all | solution.py:19
  129.5 1.7 all-to-all-done.1
  131.3 4.8 %fusion.38 = bf16[320,2304]{1,0:T(8,128)(2,1)S(1)} fusion(bf16[320,1152]{1,0:T(8,128)(2,1)S(1)} %bitcast.116, bf16[1,1152,2304]{1,2,0:T(8,128)(2,1)} %all-gather.8.cloned.1.call-done, f32[2304]{0:T(1024)S(1)} %add.105), kind=kOutput, calls=%fused_computation.41 | convolution fusion | flops 1706065920 | bytes 7529472 | tf_op jit(solution)/shard_map/dot_general | solution.py:141
  136.1 50.8 %all-gather.10.cloned.1.call-done = bf16[1,2304,1152]{2,1,0:T(8,128)(2,1)} async-done(((bf16[1,288,1152]{2,1,0:T(8,128)(2,1)}), bf16[1,2304,1152]{2,1,0:T(8,128)(2,1)}) %all-gather.10.cloned.1.call-update) | async-done | bytes 5308432 | tf_op jit(solution)/shard_map/all_gather | solution.py:150
  186.9 4.6 %fusion.53 = bf16[320,1152]{1,0:T(8,128)(2,1)S(1)} fusion(bf16[320,2304]{1,0:T(8,128)(2,1)S(1)} %fusion.38, bf16[1,2304,1152]{2,1,0:T(8,128)(2,1)} %all-gather.10.cloned.1.call-done), kind=kOutput, calls=%fused_computation.50 | convolution fusion | flops 1699061760 | bytes 7520256 | tf_op jit(solution)/shard_map/dot_general | solution.py:155
  191.5 4.3 %all_to_all.41 = bf16[2,160,1152]{2,1,0:T(8,128)(2,1)S(1)} all-to-all(bf16[2,160,1152]{2,1,0:T(8,128)(2,1)S(1)} %bitcast.118), channel_id=1, replica_groups=mesh['groups'=2,'seq'=16,'exp'=8,'tp'=2] {'tp'}, dimensions={0} | all-to-all | bytes 1474560 | tf_op jit(solution)/shard_map/all_to_all | solution.py:46
  196.7 3.6 %all-to-all-start.5 = ((bf16[2,160,1152]{2,1,0:T(8,128)(2,1)}), bf16[2,160,1152]{2,1,0:T(8,128)(2,1)S(1)}, u32[]{:S(2)}, u32[]{:S(2)}) async-start(bf16[2,160,1152]{2,1,0:T(8,128)(2,1)} %broadcast_in_dim.43), calls=%async_computation.5 | async-start | bytes 1474560 | tf_op jit(solution)/shard_map/all_to_all | solution.py:19
  200.5 1.6 all-to-all-done.5
  202.1 4.8 %fusion.50 = bf16[320,2304]{1,0:T(8,128)(2,1)S(1)} fusion(bf16[320,1152]{1,0:T(8,128)(2,1)S(1)} %bitcast.115, bf16[1,1152,2304]{1,2,0:T(8,128)(2,1)} %all-gather.8.cloned.1.call-done, f32[2304]{0:T(1024)S(1)} %add.105), kind=kOutput, calls=%fused_computation.49 | convolution fusion | flops 1706065920 | bytes 7529472 | tf_op jit(solution)/shard_map/dot_general | solution.py:141
  206.9 4.6 %fusion.56 = bf16[320,1152]{1,0:T(8,128)(2,1)S(1)} fusion(bf16[320,2304]{1,0:T(8,128)(2,1)S(1)} %fusion.50, bf16[1,2304,1152]{2,1,0:T(8,128)(2,1)} %all-gather.10.cloned.1.call-done), kind=kOutput, calls=%fused_computation.51 | convolution fusion | flops 1699061760 | bytes 7520256 | tf_op jit(solution)/shard_map/dot_general | solution.py:155
  211.6 4.3 %all_to_all.42 = bf16[2,160,1152]{2,1,0:T(8,128)(2,1)S(1)} all-to-all(bf16[2,160,1152]{2,1,0:T(8,128)(2,1)S(1)} %bitcast.117), channel_id=1, replica_groups=mesh['groups'=2,'seq'=16,'exp'=8,'tp'=2] {'tp'}, dimensions={0} | all-to-all | bytes 1474560 | tf_op jit(solution)/shard_map/all_to_all | solution.py:46
  217.3 13.1 %all-to-all-start.3 = ((bf16[16,10,1152]{2,1,0:T(8,128)(2,1)}), bf16[16,10,1152]{2,1,0:T(8,128)(2,1)S(1)}, u32[]{:S(2)}, u32[]{:S(2)}) async-start(bf16[16,10,1152]{2,1,0:T(8,128)(2,1)} %get-tuple-element.104), calls=%async_computation.3 | async-start | bytes 1179648 | tf_op jit(solution)/shard_map/all_to_all | solution.py:164
  230.7 50.2 %all-gather.6.cloned.1.call-done = bf16[4096,144]{0,1:T(8,128)(2,1)} async-done(((bf16[256,144]{0,1:T(8,128)(2,1)}), bf16[4096,144]{0,1:T(8,128)(2,1)}) %all-gather.6.cloned.1.call-update) | async-done | bytes 1179664 | tf_op jit(solution)/shard_map/all_gather | solution.py:13
  280.9 1.3 fusion.67
  283.0 7.0 %all-to-all-start.7 = ((bf16[16,10,1152]{2,1,0:T(8,128)(2,1)}), bf16[16,10,1152]{2,1,0:T(8,128)(2,1)S(1)}, u32[]{:S(2)}, u32[]{:S(2)}) async-start(bf16[16,10,1152]{2,1,0:T(8,128)(2,1)} %get-tuple-element.105), calls=%async_computation.7 | async-start | bytes 1179648 | tf_op jit(solution)/shard_map/all_to_all | solution.py:164
  290.0 5.8 %while.15 = (s32[]{:T(128)}, f32[1,256]{1,0:T(1,128)S(1)}, f32[1,256]{1,0:T(1,128)S(1)}, f32[1,256,72]{1,2,0:T(8,128)S(1)}, bf16[8,512,1,72]{1,3,2,0:T(8,128)(2,...) while((s32[]{:T(128)}, f32[1,256]{1,0:T(1,128)S(1)}, ...), condition=%wide.region_3.4_spmd.clone, body=%wide.region_0.3_spmd.clone.sunk | while | flops 38591744 | bytes 1921137 | solution.py:105
  296.4 16.1 %all-to-all-done.7 = bf16[16,10,1152]{2,1,0:T(8,128)(2,1)S(1)} async-done(((bf16[16,10,1152]{2,1,0:T(8,128)(2,1)}), bf16[16,10,1152]{2,1,0:T(8,128)(2,1)S(1)}, u32[]{:S(2)}, u32[]{:S(2)}) %all-to-all-start.7) | async-done | bytes 368672 | tf_op jit(solution)/shard_map/all_to_all | solution.py:164
  312.9 1.3 gather_fusion
  314.8 2.2 multiply_reduce_fusion
  (125 shorter events, 18.2 us)
Async XLA Ops:
  7.2 3.9 %copy-start = (bf16[128,1152]{1,0:T(8,128)(2,1)S(1)}, bf16[128,1152]{1,0:T(8,128)(2,1)}, u32[]{:S(2)}) copy-start(bf16[128,1152]{1,0:T(8,128)(2,1)} %param.21) | copy-start | bytes 884740
  7.2 124.1 %all-gather.8.cloned.1.call-start = ((), (), s32[]{:S(2)}) async-start(), calls=%async_computation.9 | async-start | bytes 5971968 | tf_op jit(solution)/shard_map/all_gather | solution.py:34
  8.0 178.9 %all-gather.10.cloned.1.call-start = ((), (), s32[]{:S(2)}) async-start(), calls=%async_computation.10 | async-start | bytes 5971968 | tf_op jit(solution)/shard_map/all_gather | solution.py:150
  11.4 83.7 %copy-start.9 = (s32[2]{0:T(128)S(1)}, s32[2]{0:T(128)}, u32[]{:S(2)}) copy-start(s32[2]{0:T(128)} %param.20) | copy-start | bytes 28
  11.5 83.7 %copy-start.2 = (bf16[256,72]{0,1:T(8,128)(2,1)S(1)}, bf16[256,72]{0,1:T(8,128)(2,1)}, u32[]{:S(2)}) copy-start(bf16[256,72]{0,1:T(8,128)(2,1)} %param.16) | copy-start | bytes 110596
  11.5 83.7 %copy-start.3 = (bf16[256,72]{0,1:T(8,128)(2,1)S(1)}, bf16[256,72]{0,1:T(8,128)(2,1)}, u32[]{:S(2)}) copy-start(bf16[256,72]{0,1:T(8,128)(2,1)} %param.18) | copy-start | bytes 110596
  11.5 83.7 %copy-start.4 = (bf16[256,72]{0,1:T(8,128)(2,1)S(1)}, bf16[256,72]{0,1:T(8,128)(2,1)}, u32[]{:S(2)}) copy-start(bf16[256,72]{0,1:T(8,128)(2,1)} %param.17) | copy-start | bytes 110596
  11.5 83.7 %copy-start.5 = (bf16[256,72]{0,1:T(8,128)(2,1)S(1)}, bf16[256,72]{0,1:T(8,128)(2,1)}, u32[]{:S(2)}) copy-start(bf16[256,72]{0,1:T(8,128)(2,1)} %param.19) | copy-start | bytes 110596
  11.7 86.2 %copy-start.7 = (f32[1,288]{1,0:T(1,128)S(1)}, f32[1,288]{1,0:T(1,128)}, u32[]{:S(2)}) copy-start(f32[1,288]{1,0:T(1,128)} %param.25) | copy-start | bytes 3460
  11.7 103.1 %copy-start.6 = (f32[1,1152]{1,0:T(1,128)S(1)}, f32[1,1152]{1,0:T(1,128)}, u32[]{:S(2)}) copy-start(f32[1,1152]{1,0:T(1,128)} %param.27) | copy-start | bytes 13828
  91.0 33.9 %all-to-all-start.4 = ((bf16[16,10,1152]{2,1,0:T(8,128)(2,1)}), bf16[16,10,1152]{2,1,0:T(8,128)(2,1)S(1)}, u32[]{:S(2)}, u32[]{:S(2)}) async-start(bf16[16,10,1152]{2,1,0:T(8,128)(2,1)} %get-tuple-element.101), calls=%async_computation.4 | async-start | bytes 1179648 | tf_op jit(solution)/shard_map/all_to_all | solution.py:53
  95.0 185.9 %all-gather.6.cloned.1.call-start = ((), (), s32[]{:S(2)}) async-start(), calls=%async_computation.8 | async-start | bytes 1253376 | tf_op jit(solution)/shard_map/all_gather | solution.py:13
  125.8 5.4 %all-to-all-start.1 = ((bf16[2,160,1152]{2,1,0:T(8,128)(2,1)}), bf16[2,160,1152]{2,1,0:T(8,128)(2,1)S(1)}, u32[]{:S(2)}, u32[]{:S(2)}) async-start(bf16[2,160,1152]{2,1,0:T(8,128)(2,1)} %broadcast_in_dim.42), calls=%async_computation.1 | async-start | bytes 1474560 | tf_op jit(solution)/shard_map/all_to_all | solution.py:19
  196.7 5.4 %all-to-all-start.5 = ((bf16[2,160,1152]{2,1,0:T(8,128)(2,1)}), bf16[2,160,1152]{2,1,0:T(8,128)(2,1)S(1)}, u32[]{:S(2)}, u32[]{:S(2)}) async-start(bf16[2,160,1152]{2,1,0:T(8,128)(2,1)} %broadcast_in_dim.43), calls=%async_computation.5 | async-start | bytes 1474560 | tf_op jit(solution)/shard_map/all_to_all | solution.py:19
  216.0 14.6 %copy-start.8 = (f32[128,2]{0,1:T(2,128)S(1)}, f32[128,2]{0,1:T(2,128)}, u32[]{:S(2)}) copy-start(f32[128,2]{0,1:T(2,128)} %param.23) | copy-start | bytes 3076
  217.3 65.7 %all-to-all-start.3 = ((bf16[16,10,1152]{2,1,0:T(8,128)(2,1)}), bf16[16,10,1152]{2,1,0:T(8,128)(2,1)S(1)}, u32[]{:S(2)}, u32[]{:S(2)}) async-start(bf16[16,10,1152]{2,1,0:T(8,128)(2,1)} %get-tuple-element.104), calls=%async_computation.3 | async-start | bytes 1179648 | tf_op jit(solution)/shard_map/all_to_all | solution.py:164
  282.2 7.8 %copy-start.1 = (bf16[256,72]{0,1:T(8,128)(2,1)S(1)}, bf16[256,72]{0,1:T(8,128)(2,1)}, u32[]{:S(2)}) copy-start(bf16[256,72]{0,1:T(8,128)(2,1)} %param.15) | copy-start | bytes 110596
  283.0 29.5 %all-to-all-start.7 = ((bf16[16,10,1152]{2,1,0:T(8,128)(2,1)}), bf16[16,10,1152]{2,1,0:T(8,128)(2,1)S(1)}, u32[]{:S(2)}, u32[]{:S(2)}) async-start(bf16[16,10,1152]{2,1,0:T(8,128)(2,1)} %get-tuple-element.105), calls=%async_computation.7 | async-start | bytes 1179648 | tf_op jit(solution)/shard_map/all_to_all | solution.py:164
Sparse Core Ops, SparseCore 0:
  10.1 103.9 all-gather.7
  116.3 70.5 all-gather.9
  189.5 91.3 all-gather.5
where the time goes:
time: 324 us
  waiting for transfers between devices  132 us (41%)
  blocking collectives  104 us (32%)
  starting transfers between devices  31.4 us (10%)
  matrix products  23.4 us (7%)
  between operations  14.9 us (5%)
  local copies, waits for them, and re-layouts  10.9 us (3%)
  other arithmetic  7.12 us (2%)
    all_to_all x1, blocking collectives, moved(): lax.all_to_all(group, axis, split_axis=split_dim, concat_axis=concat_dim,...  78.3 us
    all_gather x1, waiting for transfers between devices, expert_fn(): down_whole = lax.all_gather(down_weight[0], 'exp', axis=0, tiled=True)  50.8 us
    all_gather x1, waiting for transfers between devices, in_one_piece(): result = lax.all_gather(both, axis, axis=dim, tiled=True)  50.2 us
    all_to_all x2, starting transfers between devices, expert_fn(): lax.all_to_all(result, 'seq', split_axis=0, concat_axis=0, tiled=True)  20.1 us
    unnamed x1, blocking collectives  16.6 us
    all_to_all x2, waiting for transfers between devices, expert_fn(): lax.all_to_all(result, 'seq', split_axis=0, concat_axis=0, tiled=True)  16.1 us
    all_to_all x1, waiting for transfers between devices, moved(): lax.all_to_all(group, axis, split_axis=split_dim, concat_axis=concat_dim,...  9.91 us
    dot_general x2, matrix products, project(): jnp.dot(chip_rows, piece[0], preferred_element_type=jnp.float32) + piece[1]  9.61 us
  transfers between devices with their start and end apart: 8, of which 6 were waited for; matrix products, arithmetic and copies ran while one was open for 11% of the time, Pallas kernels for 0%

commit v1 on v0

--- a/solution.py
+++ b/solution.py
@@ -147,7 +147,9 @@
             1,
             lambda piece, start: project((piece[0], piece[1].astype(jnp.float32))),
         )
-        down_whole = lax.all_gather(down_weight[0], "exp", axis=0, tiled=True)
+        down_whole = jnp.concatenate(
+            lax.all_to_all(jnp.stack([down_weight[0]] * lax.axis_size("exp")), "exp", 0, 0), axis=0
+        )
         hidden_rows = lax.slice_in_dim(
             hidden, 0, total_rows // lax.axis_size("tp") * lax.axis_size("tp"), axis=0
         )

time: 324 us -> 426 us (1.31)
  the two profiles are of different devices: /device:TPU:68 before, /device:TPU:80 now
where the time goes in v1:
time: 426 us; the launch traced here: 425 us
  blocking collectives  244 us (57%)
  waiting for transfers between devices  87.6 us (21%)
  starting transfers between devices  37.3 us (9%)
  matrix products  21.3 us (5%)
  between operations  15.1 us (4%)
  local copies, waits for them, and re-layouts  12.8 us (3%)
  other arithmetic  7.12 us (2%)
    unnamed x1, blocking collectives  152 us
    all_to_all x1, blocking collectives, moved(): lax.all_to_all(group, axis, split_axis=split_dim, concat_axis=concat_dim,...  78.3 us
    all_gather x1, waiting for transfers between devices, in_one_piece(): result = lax.all_gather(both, axis, axis=dim, tiled=True)  33.6 us
    all_to_all x1, waiting for transfers between devices, moved(): lax.all_to_all(group, axis, split_axis=split_dim, concat_axis=concat_dim,...  31.4 us
    all_to_all x2, starting transfers between devices, expert_fn(): lax.all_to_all(result, 'seq', split_axis=0, concat_axis=0, tiled=True)  22.1 us
    all_to_all x2, waiting for transfers between devices, expert_fn(): lax.all_to_all(result, 'seq', split_axis=0, concat_axis=0, tiled=True)  20.2 us
    dot_general x2, matrix products, expert_fn(): jnp.dot(hidden_rows, down_whole, preferred_element_type=jnp.float32)  16.7 us
    all_to_all x2, blocking collectives, summed_on_arrival(): parts = lax.all_to_all(in_blocks(value, dim, size), axis, 0, 0, tiled=True)  8.63 us
  transfers between devices with their start and end apart: 7, of which 4 were waited for; matrix products, arithmetic and copies ran while one was open for 8% of the time, Pallas kernels for 0%

profile of v1, /device:TPU:80, one launch (start us, length us, event | category | flops | bytes accessed | tf_op | source)
XLA Modules:
  0.0 425.4 jit_solution(9579306577807190297)
XLA Ops:
  10.0 1.0 fusion.70
  11.0 78.3 %all_to_all.46 = bf16[16,10,1152]{2,1,0:T(8,128)(2,1)S(1)} all-to-all(bf16[16,10,1152]{2,1,0:T(8,128)(2,1)S(1)} %get-tuple-element.100), channel_id=1, replica_groups=mesh['groups'=2,'seq'=16,'exp'=8,'tp'=2] {'seq'}, dimensions={0} | all-to-all | bytes 737280 | tf_op jit(solution)/shard_map/all_to_all | solution.py:53
  89.6 4.3 %all_to_all.47 = bf16[2,160,1152]{2,1,0:T(8,128)(2,1)S(1)} all-to-all(bf16[2,160,1152]{2,1,0:T(8,128)(2,1)S(1)} %broadcast_in_dim.42), channel_id=1, replica_groups=mesh['groups'=2,'seq'=16,'exp'=8,'tp'=2] {'tp'}, dimensions={0} | all-to-all | bytes 1474560 | tf_op jit(solution)/shard_map/all_to_all | solution.py:19
  93.9 4.0 all-to-all-start.5
  98.7 31.4 %all-to-all-done.5 = bf16[16,10,1152]{2,1,0:T(8,128)(2,1)S(1)} async-done(((bf16[16,10,1152]{2,1,0:T(8,128)(2,1)}), bf16[16,10,1152]{2,1,0:T(8,128)(2,1)S(1)}, u32[]{:S(2)}, u32[]{:S(2)}) %all-to-all-start.5) | async-done | bytes 368672 | tf_op jit(solution)/shard_map/all_to_all | solution.py:53
  130.1 2.8 stack.4
  132.9 7.5 %all-to-all-start.2 = ((bf16[8,288,1152]{2,1,0:T(8,128)(2,1)}), bf16[8,288,1152]{2,1,0:T(8,128)(2,1)}, u32[]{:S(2)}, u32[]{:S(2)}) async-start(bf16[8,288,1152]{2,1,0:T(8,128)(2,1)} %stack.4), calls=%async_computation.2 | async-start | bytes 10616832 | tf_op jit(solution)/shard_map/all_to_all | solution.py:151
  141.3 1.3 dynamic-slice
  143.5 152.4 %all-reduce = bf16[2304]{0:T(1024)(128)(2,1)S(1)} all-reduce(bf16[2304]{0:T(1024)(128)(2,1)S(1)} %dynamic-update-slice), channel_id=1, replica_groups=mesh['groups'=2,'seq'=16,'exp'=8,'tp'=2] {'exp'}, use_global_device_ids=true, to_apply=%add | all-reduce | flops 2304 | bytes 9216
  296.1 8.4 %convolution_convert_fusion.1 = bf16[320,1152]{1,0:T(8,128)(2,1)S(1)} fusion(bf16[2304,1152]{1,0:T(8,128)(2,1)} %bitcast.9, bf16[320,1152]{1,0:T(8,128)(2,1)S(1)} %bitcast.112, bf16[1,1152,2304]{1,2,0:T(8,128)(2,1)} %all-gather.6.cloned.1.call-done, f32[2304]{0:T(1024)S(1)} %add.105), kind=kOutput, calls=%fused_computation.47 | convolution fusion | flops 3405127680 | bytes 12100608 | tf_op jit(solution)/shard_map/dot_general | solution.py:157
  304.5 4.3 %all_to_all.48 = bf16[2,160,1152]{2,1,0:T(8,128)(2,1)S(1)} all-to-all(bf16[2,160,1152]{2,1,0:T(8,128)(2,1)S(1)} %bitcast.115), channel_id=1, replica_groups=mesh['groups'=2,'seq'=16,'exp'=8,'tp'=2] {'tp'}, dimensions={0} | all-to-all | bytes 1474560 | tf_op jit(solution)/shard_map/all_to_all | solution.py:46
  309.7 3.6 all-to-all-start.6
  313.5 1.6 all-to-all-done.6
  315.1 8.4 %convolution_convert_fusion = bf16[320,1152]{1,0:T(8,128)(2,1)S(1)} fusion(bf16[2304,1152]{1,0:T(8,128)(2,1)} %bitcast.9, bf16[320,1152]{1,0:T(8,128)(2,1)S(1)} %bitcast.113, bf16[1,1152,2304]{1,2,0:T(8,128)(2,1)} %all-gather.6.cloned.1.call-done, f32[2304]{0:T(1024)S(1)} %add.105), kind=kOutput, calls=%fused_computation.46 | convolution fusion | flops 3405127680 | bytes 12100608 | tf_op jit(solution)/shard_map/dot_general | solution.py:157
  323.5 4.3 %all_to_all.49 = bf16[2,160,1152]{2,1,0:T(8,128)(2,1)S(1)} all-to-all(bf16[2,160,1152]{2,1,0:T(8,128)(2,1)S(1)} %bitcast.114), channel_id=1, replica_groups=mesh['groups'=2,'seq'=16,'exp'=8,'tp'=2] {'tp'}, dimensions={0} | all-to-all | bytes 1474560 | tf_op jit(solution)/shard_map/all_to_all | solution.py:46
  328.1 1.2 add_convert_fusion.1
  329.2 13.2 %all-to-all-start.4 = ((bf16[16,10,1152]{2,1,0:T(8,128)(2,1)}), bf16[16,10,1152]{2,1,0:T(8,128)(2,1)S(1)}, u32[]{:S(2)}, u32[]{:S(2)}) async-start(bf16[16,10,1152]{2,1,0:T(8,128)(2,1)} %get-tuple-element.104), calls=%async_computation.4 | async-start | bytes 1179648 | tf_op jit(solution)/shard_map/all_to_all | solution.py:166
  342.8 33.6 %all-gather.4.cloned.1.call-done = bf16[4096,144]{0,1:T(8,128)(2,1)} async-done(((bf16[256,144]{0,1:T(8,128)(2,1)}), bf16[4096,144]{0,1:T(8,128)(2,1)}) %all-gather.4.cloned.1.call-update) | async-done | bytes 1179664 | tf_op jit(solution)/shard_map/all_gather | solution.py:13
  376.5 1.3 fusion.69
  378.6 8.9 %all-to-all-start.8 = ((bf16[16,10,1152]{2,1,0:T(8,128)(2,1)}), bf16[16,10,1152]{2,1,0:T(8,128)(2,1)S(1)}, u32[]{:S(2)}, u32[]{:S(2)}) async-start(bf16[16,10,1152]{2,1,0:T(8,128)(2,1)} %get-tuple-element.105), calls=%async_computation.8 | async-start | bytes 1179648 | tf_op jit(solution)/shard_map/all_to_all | solution.py:166
  387.5 5.8 %while.15 = (s32[]{:T(128)}, f32[1,256]{1,0:T(1,128)S(1)}, f32[1,256]{1,0:T(1,128)S(1)}, f32[1,256,72]{1,2,0:T(8,128)S(1)}, bf16[8,512,1,72]{1,3,2,0:T(8,128)(2,...) while((s32[]{:T(128)}, f32[1,256]{1,0:T(1,128)S(1)}, ...), condition=%wide.region_3.4_spmd.clone, body=%wide.region_0.3_spmd.clone.sunk | while | flops 38591744 | bytes 1921137 | solution.py:105
  393.9 20.2 %all-to-all-done.8 = bf16[16,10,1152]{2,1,0:T(8,128)(2,1)S(1)} async-done(((bf16[16,10,1152]{2,1,0:T(8,128)(2,1)}), bf16[16,10,1152]{2,1,0:T(8,128)(2,1)S(1)}, u32[]{:S(2)}, u32[]{:S(2)}) %all-to-all-start.8) | async-done | bytes 368672 | tf_op jit(solution)/shard_map/all_to_all | solution.py:166
  414.5 1.3 gather_fusion
  416.3 2.2 multiply_reduce_fusion
  (124 shorter events, 14.5 us)
Async XLA Ops:
  7.2 2.3 copy-start
  89.4 40.7 %copy-start.2 = (bf16[1,288,1152]{2,1,0:T(8,128)(2,1)S(1)}, bf16[1,288,1152]{2,1,0:T(8,128)(2,1)}, u32[]{:S(2)}) copy-start(bf16[1,288,1152]{2,1,0:T(8,128)(2,1)} %param.26) | copy-start | bytes 1990660
  93.9 36.2 %all-to-all-start.5 = ((bf16[16,10,1152]{2,1,0:T(8,128)(2,1)}), bf16[16,10,1152]{2,1,0:T(8,128)(2,1)S(1)}, u32[]{:S(2)}, u32[]{:S(2)}) async-start(bf16[16,10,1152]{2,1,0:T(8,128)(2,1)} %get-tuple-element.101), calls=%async_computation.5 | async-start | bytes 1179648 | tf_op jit(solution)/shard_map/all_to_all | solution.py:53
  97.9 198.2 %all-gather.6.cloned.1.call-start = ((), (), s32[]{:S(2)}) async-start(), calls=%async_computation.10 | async-start | bytes 5971968 | tf_op jit(solution)/shard_map/all_gather | solution.py:34
  132.9 7.6 %copy-start.10 = (s32[2]{0:T(128)S(1)}, s32[2]{0:T(128)}, u32[]{:S(2)}) copy-start(s32[2]{0:T(128)} %param.20) | copy-start | bytes 28
  132.9 7.7 %copy-start.3 = (bf16[256,72]{0,1:T(8,128)(2,1)S(1)}, bf16[256,72]{0,1:T(8,128)(2,1)}, u32[]{:S(2)}) copy-start(bf16[256,72]{0,1:T(8,128)(2,1)} %param.16) | copy-start | bytes 110596
  132.9 7.7 %copy-start.4 = (bf16[256,72]{0,1:T(8,128)(2,1)S(1)}, bf16[256,72]{0,1:T(8,128)(2,1)}, u32[]{:S(2)}) copy-start(bf16[256,72]{0,1:T(8,128)(2,1)} %param.18) | copy-start | bytes 110596
  132.9 7.7 %copy-start.5 = (bf16[256,72]{0,1:T(8,128)(2,1)S(1)}, bf16[256,72]{0,1:T(8,128)(2,1)}, u32[]{:S(2)}) copy-start(bf16[256,72]{0,1:T(8,128)(2,1)} %param.17) | copy-start | bytes 110596
  132.9 7.7 %copy-start.6 = (bf16[256,72]{0,1:T(8,128)(2,1)S(1)}, bf16[256,72]{0,1:T(8,128)(2,1)}, u32[]{:S(2)}) copy-start(bf16[256,72]{0,1:T(8,128)(2,1)} %param.19) | copy-start | bytes 110596
  132.9 10.3 %copy-start.8 = (f32[1,288]{1,0:T(1,128)S(1)}, f32[1,288]{1,0:T(1,128)}, u32[]{:S(2)}) copy-start(f32[1,288]{1,0:T(1,128)} %param.25) | copy-start | bytes 3460
  132.9 163.0 %copy-start.7 = (f32[1,1152]{1,0:T(1,128)S(1)}, f32[1,1152]{1,0:T(1,128)}, u32[]{:S(2)}) copy-start(f32[1,1152]{1,0:T(1,128)} %param.27) | copy-start | bytes 13828
  132.9 163.2 %all-to-all-start.2 = ((bf16[8,288,1152]{2,1,0:T(8,128)(2,1)}), bf16[8,288,1152]{2,1,0:T(8,128)(2,1)}, u32[]{:S(2)}, u32[]{:S(2)}) async-start(bf16[8,288,1152]{2,1,0:T(8,128)(2,1)} %stack.4), calls=%async_computation.2 | async-start | bytes 10616832 | tf_op jit(solution)/shard_map/all_to_all | solution.py:151
  140.4 236.1 %all-gather.4.cloned.1.call-start = ((), (), s32[]{:S(2)}) async-start(), calls=%async_computation.9 | async-start | bytes 1253376 | tf_op jit(solution)/shard_map/all_gather | solution.py:13
  309.7 5.4 %all-to-all-start.6 = ((bf16[2,160,1152]{2,1,0:T(8,128)(2,1)}), bf16[2,160,1152]{2,1,0:T(8,128)(2,1)S(1)}, u32[]{:S(2)}, u32[]{:S(2)}) async-start(bf16[2,160,1152]{2,1,0:T(8,128)(2,1)} %broadcast_in_dim.43), calls=%async_computation.6 | async-start | bytes 1474560 | tf_op jit(solution)/shard_map/all_to_all | solution.py:19
  328.0 14.7 %copy-start.9 = (f32[128,2]{0,1:T(2,128)S(1)}, f32[128,2]{0,1:T(2,128)}, u32[]{:S(2)}) copy-start(f32[128,2]{0,1:T(2,128)} %param.23) | copy-start | bytes 3076
  329.2 49.3 %all-to-all-start.4 = ((bf16[16,10,1152]{2,1,0:T(8,128)(2,1)}), bf16[16,10,1152]{2,1,0:T(8,128)(2,1)S(1)}, u32[]{:S(2)}, u32[]{:S(2)}) async-start(bf16[16,10,1152]{2,1,0:T(8,128)(2,1)} %get-tuple-element.104), calls=%async_computation.4 | async-start | bytes 1179648 | tf_op jit(solution)/shard_map/all_to_all | solution.py:166
  377.8 9.7 %copy-start.1 = (bf16[256,72]{0,1:T(8,128)(2,1)S(1)}, bf16[256,72]{0,1:T(8,128)(2,1)}, u32[]{:S(2)}) copy-start(bf16[256,72]{0,1:T(8,128)(2,1)} %param.15) | copy-start | bytes 110596
  378.6 35.5 %all-to-all-start.8 = ((bf16[16,10,1152]{2,1,0:T(8,128)(2,1)}), bf16[16,10,1152]{2,1,0:T(8,128)(2,1)S(1)}, u32[]{:S(2)}, u32[]{:S(2)}) async-start(bf16[16,10,1152]{2,1,0:T(8,128)(2,1)} %get-tuple-element.105), calls=%async_computation.8 | async-start | bytes 1179648 | tf_op jit(solution)/shard_map/all_to_all | solution.py:166
Sparse Core Ops, SparseCore 0:
  100.8 148.1 all-gather.5
  251.7 124.7 all-gather.3
